TPU v7x, 32 devices: a whole 2x2x4 slice. The times are simulated.
32 devices in a mesh: rep: 16 (over z, y, core), tp: 2 (over x).
Axes of the slice: x: 2, y: 2, z: 4, core: 2. Of those that a mesh axis runs over, the one named last changes fastest.
Arguments:
- context: bfloat16 [4096, 3072], P('rep', 'tp'), may hold values from -6 to 6
- residual: bfloat16 [4096, 5120], P(('rep', 'tp')), may hold values from -6 to 6
- cotangent: bfloat16 [4096, 5120], P(('rep', 'tp')), may hold values from -6 to 6
- numer: bfloat16 [16, 3072, 5120], P('rep', 'tp'), may hold values from -0.109375 to 0.109375
- weight: float32 [16], P('rep'), may hold values from 0.5 to 2
- step: int32 [1], replicated, may hold values from 0 to 999999
Outputs:
- output: bfloat16 [4096, 5120], P(('rep', 'tp'))
- grad_context: bfloat16 [4096, 3072], P('rep', 'tp')
- numer_next: bfloat16 [16, 3072, 5120], P('rep', 'tp')
- weight_next: float32 [16], P('rep')
All inputs are finite; a program needn't handle non-finite values.
Results may differ from a plain program's by a relative error of at most 0.013.
Values may be sent and summed in bfloat16 or wider, within the bound.
No kernel may reach another device: no remote copies, remote signals or barrier semaphores. Data moves between devices by JAX's collectives and lax.ppermute only.
A program may use at most 192 MiB of HBM per device.

v0:
```python
from functools import partial

import jax
import jax.numpy as jnp
from jax import lax
from jax.sharding import PartitionSpec as P

PEER_BITS = 3


LEARN = 0.001


def for_sending(array):

    def short(part):
        return part.astype(jnp.bfloat16) if part.dtype == jnp.float32 else part

    return jax.tree.map(short, array)


def from_behind(block, axis, distance):
    devices = range(lax.axis_size(axis))
    route = [((i - distance) % len(devices), i) for i in devices]
    return lax.ppermute(block, axis, route)


def move_peer(bits, pair):
    return jax.tree.map(
        lambda part, own: part.astype(own.dtype),
        from_behind(for_sending(pair), "rep", 1 << bits),
        pair,
    )


def on_device(context, residual, cotangent, numer, weight, step):
    own_numer = numer[0]
    params = (own_numer.astype(jnp.float32) / weight[0]).astype(jnp.bfloat16)
    block = context
    summed = lax.psum_scatter(
        jnp.dot(block, params, preferred_element_type=jnp.float32).astype(jnp.bfloat16),
        "tp",
        scatter_dimension=0,
        tiled=True,
    ).astype(jnp.float32)
    output = (residual.astype(jnp.float32) + summed).astype(jnp.bfloat16)
    piece = lax.all_gather(cotangent, "tp", axis=0, tiled=True)
    block = context
    grad_w = lax.dot_general(
        block, piece, (((0,), (0,)), ((), ())), preferred_element_type=jnp.float32
    )
    rows = lax.dot_general(
        piece, params, (((1,), (1,)), ((), ())), preferred_element_type=jnp.float32
    )
    grad_ctx = rows
    grad_w, grad_ctx = (grad_w, grad_ctx)
    exponent = jnp.remainder(step[0], jnp.int32(PEER_BITS + 1))
    branches = [partial(move_peer, bits) for bits in range(PEER_BITS + 1)]
    peer_numer, peer_weight = lax.switch(exponent, branches, (numer, weight))
    mixed = (
        0.5 * (own_numer.astype(jnp.float32) + peer_numer[0].astype(jnp.float32)) - LEARN * grad_w
    )
    numer_next = mixed.astype(jnp.bfloat16)[None]
    weight_next = 0.5 * (weight + peer_weight)
    return (output, grad_ctx.astype(jnp.bfloat16), numer_next, weight_next)


def solution(mesh):
    in_specs = (
        P("rep", "tp"),
        P(("rep", "tp"), None),
        P(("rep", "tp"), None),
        P("rep", "tp", None),
        P("rep"),
        P(),
    )
    out_specs = (P(("rep", "tp"), None), P("rep", "tp"), P("rep", "tp", None), P("rep"))
    return jax.shard_map(
        on_device, mesh=mesh, in_specs=in_specs, out_specs=out_specs, check_vma=False
    )
```

profile of v0, /device:TPU:0, one launch (start us, length us, event | category | flops | bytes accessed | tf_op | source)
XLA Modules:
  0.0 436.6 jit_solution(1694881537635788757)
XLA Ops:
  7.2 0.0 copy-start
  7.2 0.0 all-gather.2.cloned.1.call-start
  7.2 0.7 all-gather.2.cloned.1.call-update
  7.9 0.0 reduce-scatter.4.cloned.1.call-start
  8.6 8.8 %fusion = bf16[1536,5120]{1,0:T(8,128)(2,1)S(1)} fusion(bf16[1,1536,5120]{2,1,0:T(8,128)(2,1)} %param.13, f32[]{:T(128)} %bitcast.31), kind=kLoop, calls=%fused_computation.6 | loop fusion | flops 23592960 | bytes 31457284 | tf_op jit(solution)/shard_map/convert_element_type | solution.py:38
  17.4 0.0 copy-start.1
  17.4 6.4 %copy-done.1 = bf16[1536,5120]{1,0:T(8,128)(2,1)} copy-done((bf16[1536,5120]{1,0:T(8,128)(2,1)}, bf16[1536,5120]{1,0:T(8,128)(2,1)S(1)}, u32[]{:S(2)}) %copy-start.1) | copy-done | bytes 15728664
  23.9 0.0 copy-done
  23.9 4.8 %fusion.5 = bf16[256,5120]{0,1:T(8,128)(2,1)S(1)} fusion(bf16[1536,5120]{1,0:T(8,128)(2,1)S(1)} %fusion, bf16[256,1536]{1,0:T(8,128)(2,1)S(1)} %copy-done), kind=kOutput, calls=%fused_computation.12 | convolution fusion | flops 4027842560 | bytes 19136512 | tf_op jit(solution)/shard_map/dot_general | solution.py:41
  28.7 2.9 copy.16
  31.6 0.0 reduce-scatter.4.cloned.1.call-update
  32.3 0.0 copy-start.2
  32.3 353.7 %conditional.4 = (f32[1536,5120]{1,0:T(8,128)}, bf16[1]{0:T(256)(128)(2,1)}) conditional(s32[]{:T(128)} %clamp.3, (f32[1]{0:T(128)}, bf16[1,1536,5120]{2,1,0:T(8,128)(2,1)}) %tuple.46, (f32[1]{0:T(128)}, bf16[1,1536,5120]{2,1,0:T(8,128)(2,1)}) %tuple.46, (f32[1]{0:T(128)}, ...), branch_computations={%region_1.2_spmd, %region_2.3_spmd, %region_3.4_spmd, %region_4.5_... | conditional | flops 7864321 | bytes 110100592
  32.3 2.8 collective-permute-start.5
  35.8 336.8 %collective-permute-start.4 = (bf16[1]{0:T(256)(128)(2,1)}, bf16[1]{0:T(256)(128)(2,1)}, u32[]{:S(2)}, u32[]{:S(2)}) collective-permute-start(bf16[1]{0:T(256)(128)(2,1)} %convert_element_type.56), channel_id=1, source_target_pairs={{24,0},{26,2},{28,4},{30,6},{0,8},{2,10},{4,12},{6,14},{8,16},{10,... | collective-permute-start | bytes 14 | tf_op jit(solution)/shard_map/cond/branch_2_fun/ppermute | solution.py:25
  372.5 2.6 collective-permute-done.5
  375.2 10.8 %bitcast_convert_fusion.2 = f32[1536,5120]{1,0:T(8,128)} fusion(bf16[1,1536,5120]{2,1,0:T(8,128)(2,1)S(1)} %collective-permute-done.5), kind=kLoop, calls=%fused_computation.2 | loop fusion | flops 7864320 | bytes 47185920 | tf_op jit(solution)/shard_map/convert_element_type | solution.py:61
  386.0 0.0 collective-permute-done.4
  386.5 0.0 copy-done.2
  386.6 0.8 copy.13
  387.3 0.0 all-gather.2.cloned.1.call-done
  387.4 10.6 %fusion.6 = bf16[256,1536]{0,1:T(8,128)(2,1)S(1)} fusion(bf16[1536,5120]{1,0:T(8,128)(2,1)} %copy-done.1, bf16[256,5120]{1,0:T(8,128)(2,1)} %all-gather.2.cloned.1.call-done), kind=kOutput, calls=%fused_computation.15 | convolution fusion | flops 4026925056 | bytes 19136512 | tf_op jit(solution)/shard_map/dot_general | solution.py:52
  398.0 1.2 copy.15
  399.1 23.9 %fusion.4 = bf16[1,1536,5120]{2,1,0:T(8,128)(2,1)} fusion(bf16[256,1536]{1,0:T(8,128)(2,1)S(1)} %copy-done, bf16[256,5120]{1,0:T(8,128)(2,1)} %all-gather.2.cloned.1.call-done, f32[1536,5120]{1,0:T(8,128)} %get-tuple-element.43, bf16[1,1536,5120]{2,1,0:T(8,128)(2,1)} %param.13), kind=kOutput, calls=%fused_computation.10 | convolution fusion | flops 4073717760 | bytes 66322432 | tf_op jit(solution)/shard_map/dot_general | solution.py:49
  423.0 0.0 reduce-scatter.4.cloned.1.call-done
  423.0 1.8 copy.17
  424.8 1.4 add_convert_fusion
  426.2 2.4 copy.14
Async XLA Ops:
  7.2 16.7 %copy-start = (bf16[256,1536]{1,0:T(8,128)(2,1)S(1)}, bf16[256,1536]{1,0:T(8,128)(2,1)}, u32[]{:S(2)}) copy-start(bf16[256,1536]{1,0:T(8,128)(2,1)} %param.10) | copy-start | bytes 2359300
  7.2 380.2 %all-gather.2.cloned.1.call-start = ((), (), s32[]{:S(2)}) async-start(), calls=%async_computation.1 | async-start | bytes 3932160 | tf_op jit(solution)/shard_map/all_gather | solution.py:47
  7.9 415.1 %reduce-scatter.4.cloned.1.call-start = ((), (), s32[]{:S(2)}) async-start(), calls=%async_computation.2 | async-start | bytes 3932160
  17.4 6.4 %copy-start.1 = (bf16[1536,5120]{1,0:T(8,128)(2,1)}, bf16[1536,5120]{1,0:T(8,128)(2,1)S(1)}, u32[]{:S(2)}) copy-start(bf16[1536,5120]{1,0:T(8,128)(2,1)S(1)} %fusion) | copy-start | bytes 47185924
  32.3 354.3 %copy-start.2 = (bf16[128,5120]{1,0:T(8,128)(2,1)S(1)}, bf16[128,5120]{1,0:T(8,128)(2,1)}, u32[]{:S(2)}) copy-start(bf16[128,5120]{1,0:T(8,128)(2,1)} %param.11) | copy-start | bytes 3932164
  32.3 342.8 %collective-permute-start.5 = (bf16[1,1536,5120]{2,1,0:T(8,128)(2,1)}, bf16[1,1536,5120]{2,1,0:T(8,128)(2,1)S(1)}, u32[]{:S(2)}, u32[]{:S(2)}) collective-permute-start(bf16[1,1536,5120]{2,1,0:T(8,128)(2,1)} %get-tuple-element.32), channel_id=1, source_target_pairs={{24,0},{26,2},{28,4},{30,6},{0,8},{2,10},{4,12},{6,14},{8,16},{10,... | collective-permute-start | bytes 47185928 | tf_op jit(solution)/shard_map/cond/branch_2_fun/ppermute | solution.py:25
  35.8 350.2 %collective-permute-start.4 = (bf16[1]{0:T(256)(128)(2,1)}, bf16[1]{0:T(256)(128)(2,1)}, u32[]{:S(2)}, u32[]{:S(2)}) collective-permute-start(bf16[1]{0:T(256)(128)(2,1)} %convert_element_type.56), channel_id=1, source_target_pairs={{24,0},{26,2},{28,4},{30,6},{0,8},{2,10},{4,12},{6,14},{8,16},{10,... | collective-permute-start | bytes 14 | tf_op jit(solution)/shard_map/cond/branch_2_fun/ppermute | solution.py:25
Sparse Core Ops, SparseCore 0:
  9.5 41.7 all-gather.1
  53.5 37.6 reduce-scatter.3
where the time goes:
time: 437 us
  starting transfers between devices  340 us (78%)
  matrix products  39.3 us (9%)
  other arithmetic  21 us (5%)
  between operations  17.1 us (4%)
  local copies, waits for them, and re-layouts  15.5 us (4%)
    ppermute x2, starting transfers between devices, from_behind(): return lax.ppermute(block, axis, route)  340 us
    dot_general x1, matrix products, on_device(): lax.dot_general(block, piece, (((0,), (0,)), ((), ())), preferred_element...  23.9 us
    unnamed x11, local copies, waits for them, and re-layouts  15.5 us
    convert_element_type x1, other arithmetic, on_device(): peer_numer[0].astype(jnp.float32)  10.8 us
    dot_general x1, matrix products, on_device(): lax.dot_general(piece, params, (((1,), (1,)), ((), ())), preferred_elemen...  10.6 us
    convert_element_type x1, other arithmetic, on_device(): params = (own_numer.astype(jnp.float32) / weight[0]).astype(jnp.bfloat16)  8.8 us
  transfers between devices with their start and end apart: 4, of which 1 were waited for; matrix products, arithmetic and copies ran while one was open for 15% of the time, Pallas kernels for 0%

commit v1 on v0

v1 whole, which is shorter than its diff:
```python
from functools import partial

import jax
import jax.numpy as jnp
from jax import lax
from jax.experimental import pallas as pl
from jax.experimental.layout import Layout, with_layout_constraint
from jax.experimental.pallas import tpu as pltpu
from jax.sharding import PartitionSpec as P

PEER_BITS = 3


LEARN = 0.001


PIECES = ((23, 1), (0, 8), (8, 12), (20, 2), (22, 1))


def pieces_of(rows):
    if rows % (24 * 16):
        return ((0, rows),)
    unit = rows // 24
    return tuple((start * unit, size * unit) for start, size in PIECES)


def from_behind(block, axis, distance):
    devices = range(lax.axis_size(axis))
    route = [((i - distance) % len(devices), i) for i in devices]
    return lax.ppermute(block, axis, route)


def mix_body(ctx_ref, cot_ref, own_ref, peer_ref, *rest):
    out_ref = rest[-1]
    width = out_ref.shape[1]
    tile = 512 if width % 512 == 0 else width

    @pl.loop(0, width // tile)
    def _(j):
        cols = pl.ds(pl.multiple_of(j * tile, tile), tile)
        grad = jnp.dot(ctx_ref[...], cot_ref[:, cols], preferred_element_type=jnp.float32)
        both = own_ref[:, cols].astype(jnp.float32) + peer_ref[:, cols].astype(jnp.float32)
        out_ref[:, cols] = (0.5 * both - LEARN * grad).astype(out_ref.dtype)


def mix_rows(start, size, ctx_t, cot, own, peer, so_far):
    rows, width = own.shape
    tokens = cot.shape[0]
    block = next(b for b in (128, 64, 32, 16, 8, size) if size % b == 0 and start % b == 0)
    first = start // block
    in_specs = [
        pl.BlockSpec((block, tokens), lambda i: (first + i, 0)),
        pl.BlockSpec((tokens, width), lambda i: (0, 0)),
        pl.BlockSpec((block, width), lambda i: (first + i, 0)),
        pl.BlockSpec((block, width), lambda i: (i, 0)),
    ]
    operands = [ctx_t, cot, own, peer]
    aliases = {}
    if so_far is not None:
        in_specs.append(pl.BlockSpec(memory_space=pl.ANY))
        operands.append(so_far)
        aliases = {4: 0}
    return pl.pallas_call(
        mix_body,
        grid=(size // block,),
        in_specs=in_specs,
        out_specs=pl.BlockSpec((block, width), lambda i: (first + i, 0)),
        out_shape=jax.ShapeDtypeStruct((rows, width), own.dtype),
        input_output_aliases=aliases,
        compiler_params=pltpu.CompilerParams(vmem_limit_bytes=24 * 2**20),
        cost_estimate=pl.CostEstimate(
            flops=2 * size * tokens * width, bytes_accessed=6 * size * width, transcendentals=0
        ),
    )(*operands)


def tail_base(start, size, ctx_t, cot, own):
    grad = jnp.dot(ctx_t[start : start + size], cot, preferred_element_type=jnp.float32)
    return 0.5 * own[start : start + size].astype(jnp.float32) - LEARN * grad


def step_at(bits, context, residual, cotangent, numer, weight):
    distance = 1 << bits
    own_numer = numer[0]
    pieces = pieces_of(own_numer.shape[0])
    peer_weight = from_behind(weight, "rep", distance)
    arrived = []
    source = own_numer
    for start, size in pieces:
        piece = lax.slice_in_dim(source, start, start + size, axis=0)
        source, piece = lax.optimization_barrier((source, piece))
        arrived.append(from_behind(piece, "rep", distance))

    share = lax.axis_size("tp")
    place = lax.axis_index("tp")
    tokens = cotangent.shape[0]
    cot = jnp.zeros((share * tokens, cotangent.shape[1]), cotangent.dtype)
    for away in range(share):
        rows = from_behind(cotangent, "tp", away) if away else cotangent
        cot = lax.dynamic_update_slice(
            cot, rows, (lax.rem(place - away + share, share) * tokens, 0)
        )

    params = (own_numer.astype(jnp.float32) / weight[0]).astype(jnp.bfloat16)
    projected = jnp.dot(context, params, preferred_element_type=jnp.float32)
    total = lax.dynamic_slice_in_dim(projected, place * tokens, tokens, axis=0)
    for away in range(1, share):
        target = lax.rem(place + away, share)
        rows = lax.dynamic_slice_in_dim(projected, target * tokens, tokens, axis=0)
        rows = from_behind(rows.astype(jnp.bfloat16), "tp", away)
        total = total + rows.astype(jnp.float32)
    output = (residual.astype(jnp.float32) + total).astype(jnp.bfloat16)
    output = with_layout_constraint(output, Layout(major_to_minor=(0, 1)))

    grad_ctx = lax.dot_general(
        cot, params, (((1,), (1,)), ((), ())), preferred_element_type=jnp.float32
    ).astype(jnp.bfloat16)

    ctx_t = context.T
    base = tail_base(*pieces[-1], ctx_t, cot, own_numer)
    numer_next = None
    for (start, size), peer in zip(pieces[:-1], arrived[:-1]):
        if numer_next is not None:
            numer_next, peer = lax.optimization_barrier((numer_next, peer))
        numer_next = mix_rows(start, size, ctx_t, cot, own_numer, peer, numer_next)
    numer_next, base, peer_weight = lax.optimization_barrier((numer_next, base, peer_weight))
    weight_next = 0.5 * (weight + peer_weight)
    last = (base + 0.5 * arrived[-1].astype(jnp.float32)).astype(jnp.bfloat16)
    numer_next = lax.dynamic_update_slice(numer_next, last, (pieces[-1][0], 0))
    return output, grad_ctx, numer_next[None], weight_next


def branch(bits, *operands):
    return step_at(bits, *operands)


def on_device(context, residual, cotangent, numer, weight, step):
    exponent = jnp.remainder(step[0], jnp.int32(PEER_BITS + 1))
    branches = [partial(branch, bits) for bits in range(PEER_BITS + 1)]
    return lax.switch(exponent, branches, context, residual, cotangent, numer, weight)


def solution(mesh):
    in_specs = (
        P("rep", "tp"),
        P(("rep", "tp"), None),
        P(("rep", "tp"), None),
        P("rep", "tp", None),
        P("rep"),
        P(),
    )
    out_specs = (P(("rep", "tp"), None), P("rep", "tp"), P("rep", "tp", None), P("rep"))
    return jax.shard_map(
        on_device, mesh=mesh, in_specs=in_specs, out_specs=out_specs, check_vma=False
    )
```

time: 437 us -> 351 us (0.80)
  starting transfers between devices: 340 us -> 11.7 us
  waiting for transfers between devices: 3.34 us -> 242 us
  Pallas kernels: 0 us -> 33.8 us
  matrix products: 39.3 us -> 17.2 us
  between operations: 17.1 us -> 2.42 us
  local copies, waits for them, and re-layouts: 15.5 us -> 26.4 us
  other arithmetic: 21 us -> 14.5 us
    ppermute x2 -> x8, starting transfers between devices: 340 us -> 11.7 us  [from_behind(): return lax.ppermute(block, axis, route)]
    ppermute x2 -> x8, waiting for transfers between devices: 2.62 us -> 242 us  [from_behind(): return lax.ppermute(block, axis, route)]
    pallas_call x0 -> x4, Pallas kernels: none -> 33.8 us  [mix_rows(): pl.pallas_call(mix_body, grid=(size // block,), in_specs=in_specs, out_sp...]
    dot_general x3, matrix products: 39.3 us -> 17.2 us  [the longest x1 8.65 us: step_at(): lax.dot_general(cot, params, (((1,), (1,)), ((), ())), preferred_element_...]
    slice x0 -> x5, local copies, waits for them, and re-layouts: none -> 18.5 us  [step_at(): piece = lax.slice_in_dim(source, start, start + size, axis=0)]
    unnamed x11 -> x12, local copies, waits for them, and re-layouts: 15.5 us -> 0.35 us
    convert_element_type x3 -> x1, other arithmetic: 21 us -> 9.52 us  [step_at(): params = (own_numer.astype(jnp.float32) / weight[0]).astype(jnp.bfloat16)]
  transfers between devices with their start and end apart: 4 -> 8, of which waited for: 1 -> 5; matrix products, arithmetic and copies ran while one was open for 15% -> 16% of each run, Pallas kernels for 0% -> 10%
where the time goes in v1:
time: 351 us; the launch traced here: 350 us
  waiting for transfers between devices  242 us (69%)
  Pallas kernels  33.8 us (10%)
  local copies, waits for them, and re-layouts  26.4 us (8%)
  matrix products  17.2 us (5%)
  other arithmetic  14.5 us (4%)
  starting transfers between devices  11.7 us (3%)
    ppermute x8, waiting for transfers between devices, from_behind(): return lax.ppermute(block, axis, route)  242 us
    pallas_call x4, Pallas kernels, mix_rows(): pl.pallas_call(mix_body, grid=(size // block,), in_specs=in_specs, out_sp...  33.8 us
    slice x5, local copies, waits for them, and re-layouts, step_at(): piece = lax.slice_in_dim(source, start, start + size, axis=0)  18.5 us
    ppermute x8, starting transfers between devices, from_behind(): return lax.ppermute(block, axis, route)  11.7 us
    convert_element_type x1, other arithmetic, step_at(): params = (own_numer.astype(jnp.float32) / weight[0]).astype(jnp.bfloat16)  9.52 us
    dot_general x1, matrix products, step_at(): lax.dot_general(cot, params, (((1,), (1,)), ((), ())), preferred_element_...  8.65 us
  transfers between devices with their start and end apart: 8, of which 5 were waited for; matrix products, arithmetic and copies ran while one was open for 16% of the time, Pallas kernels for 10%

profile of v1, /device:TPU:0, one launch (start us, length us, event | category | flops | bytes accessed | tf_op | source)
XLA Modules:
  0.0 350.0 jit_solution(11872120633743803086)
XLA Ops:
  1.3 347.6 %conditional.3 = (bf16[128,5120]{1,0:T(8,128)(2,1)}, bf16[256,1536]{1,0:T(8,128)(2,1)}, bf16[1,1536,5120]{2,1,0:T(8,128)(2,1)}, f32[1]{0:T(128)}) conditional(s32[]{:T(128)} %clamp.3, (bf16[128,5120]{1,0:T(8,128)(2,1)}, bf16[1,1536,5120]{2,1,0:T(8,128)(2,1)}, f32[1]{0:T(128)}, bf16[256,1536]{1,0:T(8,128)(2,1)}, ...), branch_computations={%region_0.1_spmd, %region_1.2_spmd, %region_2.3_spmd, %region_3.4_... | conditional | flops 12109086720 | bytes 361530176
  1.6 3.0 collective-permute-start.17
  4.6 2.0 slice_bitcast_fusion.2
  6.6 1.6 collective-permute-start.18
  8.2 5.2 %slice.86 = bf16[512,5120]{1,0:T(8,128)(2,1)} slice(bf16[1536,5120]{1,0:T(8,128)(2,1)} %bitcast.156), slice={[0:512], [0:5120]} | slice | bytes 10485760 | tf_op jit(solution)/shard_map/cond/branch_2_fun/slice | solution.py:90
  13.4 1.6 collective-permute-start.19
  15.0 6.8 %slice.87 = bf16[768,5120]{1,0:T(8,128)(2,1)} slice(bf16[1536,5120]{1,0:T(8,128)(2,1)} %bitcast.157), slice={[512:1280], [0:5120]} | slice | bytes 15728640 | tf_op jit(solution)/shard_map/cond/branch_2_fun/slice | solution.py:90
  21.8 1.6 collective-permute-start.20
  23.3 0.2 collective-permute-start.22
  23.6 0.0 copy-start.6
  23.6 9.5 %divide_convert_fusion.2 = bf16[1536,5120]{1,0:T(8,128)(2,1)S(1)} fusion(f32[]{:T(128)} %bitcast.21, bf16[1,1536,5120]{2,1,0:T(8,128)(2,1)} %get-tuple-element.92), kind=kLoop, calls=%fused_computation.30 | loop fusion | flops 23592960 | bytes 31457284 | tf_op jit(solution)/shard_map/cond/branch_2_fun/convert_element_type | solution.py:104
  33.1 0.0 copy-start.2
  33.1 0.0 copy-done.6
  33.1 6.7 %fusion.33 = f32[5120,256]{0,1:T(8,128)} fusion(bf16[256,1536]{1,0:T(8,128)(2,1)S(1)} %copy-done.6, bf16[1536,5120]{1,0:T(8,128)(2,1)S(1)} %divide_convert_fusion.2), kind=kOutput, calls=%fused_computation.65 | convolution fusion | flops 4026531840 | bytes 21757952 | tf_op jit(solution)/shard_map/cond/branch_2_fun/dot_general | solution.py:105
  39.8 0.3 copy-done.2
  40.2 0.3 broadcast.65
  40.5 1.5 constant_dynamic-update-slice_fusion.5
  41.9 3.0 fusion.17
  44.9 1.4 copy.32
  46.3 2.5 slice.88
  48.8 2.0 slice.91
  50.8 0.0 collective-permute-done.17
  50.8 1.6 collective-permute-start.21
  52.4 1.5 constant_dynamic-update-slice_fusion.4.cot_ref
  53.8 0.0 collective-permute-done.18.peer_ref
  53.8 0.6 collective-permute-start.16
  54.4 3.9 %branch_2_fun.4.rest_0_ = bf16[1536,5120]{1,0:T(8,128)(2,1)} custom-call(bf16[1536,256]{1,0:T(8,128)(2,1)S(1)} %bitcast.126, bf16[256,5120]{1,0:T(8,128)(2,1)S(1)} %constant_dynamic-update-slice_fusion.4.cot_ref, bf16[1536,5120]{1,0:T(8,128)(2,1)} %bitcast.160, bf16[64,5120]{1,0:T(8,128)(2,1)} %collective-permute-done.18.peer_ref), custom_call_target="tpu_custom_call" | custom-call | flops 167772160 | bytes 1966080 | tf_op jit(solution)/shard_map/cond/branch_2_fun/pallas_call | solution.py:63
  58.3 8.6 %fusion.32 = bf16[256,1536]{1,0:T(8,128)(2,1)} fusion(bf16[256,5120]{1,0:T(8,128)(2,1)S(1)} %constant_dynamic-update-slice_fusion.4.cot_ref, bf16[1536,5120]{1,0:T(8,128)(2,1)} %copy-done.2), kind=kOutput, calls=%fused_computation.64 | convolution fusion | flops 4026531840 | bytes 19136512 | tf_op jit(solution)/shard_map/cond/branch_2_fun/dot_general | solution.py:115
  67.0 16.1 %collective-permute-done.16 = bf16[128,5120]{1,0:T(8,128)(2,1)} collective-permute-done((bf16[128,5120]{1,0:T(8,128)(2,1)}, bf16[128,5120]{1,0:T(8,128)(2,1)}, u32[]{:S(2)}, u32[]{:S(2)}) %collective-permute-start.16) | collective-permute-done | bytes 1310752 | tf_op jit(solution)/shard_map/cond/branch_2_fun/ppermute | solution.py:30
  83.0 1.6 collective-permute-start.23
  84.6 4.0 %fusion.16 = bf16[128,5120]{1,0:T(8,128)(2,1)} fusion(bf16[128,5120]{1,0:T(8,128)(2,1)} %collective-permute-done.16, f32[5120,256]{0,1:T(8,128)} %fusion.33, s32[]{:T(128)S(6)} %select_n.40, bf16[128,5120]{1,0:T(8,128)(2,1)} %get-tuple-element.91), kind=kLoop, calls=%fused_computation.35 | loop fusion | flops 3276800 | bytes 6553604 | tf_op jit(solution)/shard_map/cond/branch_2_fun/add | solution.py:112
  88.6 1.8 fusion.15
  90.5 0.0 slice-start.9
  90.5 0.0 slice-start.10
  90.5 0.0 slice-start.11
  90.5 48.1 %collective-permute-done.19.peer_ref = bf16[512,5120]{1,0:T(8,128)(2,1)} collective-permute-done((bf16[512,5120]{1,0:T(8,128)(2,1)}, bf16[512,5120]{1,0:T(8,128)(2,1)}, u32[]{:S(2)}, u32[]{:S(2)}) %collective-permute-start.19) | collective-permute-done | bytes 5242912 | tf_op jit(solution)/shard_map/cond/branch_2_fun/ppermute | solution.py:30
  138.6 11.0 %branch_2_fun.5.rest_0_ = bf16[1536,5120]{1,0:T(8,128)(2,1)} custom-call(bf16[1536,256]{1,0:T(8,128)(2,1)S(1)} %bitcast.128, bf16[256,5120]{1,0:T(8,128)(2,1)S(1)} %constant_dynamic-update-slice_fusion.4.cot_ref, bf16[1536,5120]{1,0:T(8,128)(2,1)} %bitcast.161, bf16[512,5120]{1,0:T(8,128)(2,1)} %collective-permute-done.19.peer_ref, ...), custom_call_target="tpu_custom_call", output_to_operand_aliasing={{}: (4, {})} | custom-call | flops 1342177280 | bytes 15728640 | tf_op jit(solution)/shard_map/cond/branch_2_fun/pallas_call | solution.py:63
  149.7 157.5 %collective-permute-done.20.peer_ref = bf16[768,5120]{1,0:T(8,128)(2,1)} collective-permute-done((bf16[768,5120]{1,0:T(8,128)(2,1)}, bf16[768,5120]{1,0:T(8,128)(2,1)}, u32[]{:S(2)}, u32[]{:S(2)}) %collective-permute-start.20) | collective-permute-done | bytes 7864352 | tf_op jit(solution)/shard_map/cond/branch_2_fun/ppermute | solution.py:30
  307.2 0.0 slice-done.8
  307.2 0.0 slice-done.9
  307.2 0.0 slice-done.10
  307.2 0.0 slice-done.11
  307.2 14.5 %branch_2_fun.6.rest_0_ = bf16[1536,5120]{1,0:T(8,128)(2,1)} custom-call(bf16[1536,256]{1,0:T(8,128)(2,1)S(1)} %bitcast.129, bf16[256,5120]{1,0:T(8,128)(2,1)S(1)} %constant_dynamic-update-slice_fusion.4.cot_ref, bf16[1536,5120]{1,0:T(8,128)(2,1)S(1)} %bitcast.164, ...), custom_call_target="tpu_custom_call", output_to_operand_aliasing={{}: (4, {})} | custom-call | flops 2013265920 | bytes 23592960 | tf_op jit(solution)/shard_map/cond/branch_2_fun/pallas_call | solution.py:63
  321.7 13.6 %collective-permute-done.21.peer_ref = bf16[128,5120]{1,0:T(8,128)(2,1)} collective-permute-done((bf16[128,5120]{1,0:T(8,128)(2,1)}, bf16[128,5120]{1,0:T(8,128)(2,1)}, u32[]{:S(2)}, u32[]{:S(2)}) %collective-permute-start.21) | collective-permute-done | bytes 1310752 | tf_op jit(solution)/shard_map/cond/branch_2_fun/ppermute | solution.py:30
  335.3 4.4 %branch_2_fun.7 = bf16[1536,5120]{1,0:T(8,128)(2,1)} custom-call(bf16[1536,256]{1,0:T(8,128)(2,1)S(1)} %bitcast.130, bf16[256,5120]{1,0:T(8,128)(2,1)S(1)} %constant_dynamic-update-slice_fusion.4.cot_ref, bf16[1536,5120]{1,0:T(8,128)(2,1)S(1)} %bitcast.165, bf16[128,5120]{1,0:T(8,128)(2,1)} %collective-permute-done.21.peer_ref, ...), custom_call_target="tpu_custom_call", output_to_operand_aliasing={{}: (4, {})} | custom-call | flops 335544320 | bytes 3932160 | tf_op jit(solution)/shard_map/cond/branch_2_fun/pallas_call | solution.py:63
  339.7 0.0 collective-permute-done.22
  340.9 7.0 %collective-permute-done.23 = bf16[64,5120]{1,0:T(8,128)(2,1)S(1)} collective-permute-done((bf16[64,5120]{1,0:T(8,128)(2,1)}, bf16[64,5120]{1,0:T(8,128)(2,1)S(1)}, u32[]{:S(2)}, u32[]{:S(2)}) %collective-permute-start.23) | collective-permute-done | bytes 655392 | tf_op jit(solution)/shard_map/cond/branch_2_fun/ppermute | solution.py:30
  347.9 1.0 fusion.19
  (2 shorter events, 0.0 us)
Async XLA Ops:
  1.6 49.2 %collective-permute-start.17 = (bf16[128,5120]{1,0:T(8,128)(2,1)}, bf16[128,5120]{1,0:T(8,128)(2,1)}, u32[]{:S(2)}, u32[]{:S(2)}) collective-permute-start(bf16[128,5120]{1,0:T(8,128)(2,1)} %get-tuple-element.95), channel_id=1, source_target_pairs={{1,0},{0,1},{3,2},{2,3},{5,4},{4,5},{7,6},{6,7},{9,8},{8,9},{11,10... | collective-permute-start | bytes 3932168 | tf_op jit(solution)/shard_map/cond/branch_2_fun/ppermute | solution.py:30
  6.6 47.2 %collective-permute-start.18 = (bf16[64,5120]{1,0:T(8,128)(2,1)}, bf16[64,5120]{1,0:T(8,128)(2,1)}, u32[]{:S(2)}, u32[]{:S(2)}) collective-permute-start(bf16[64,5120]{1,0:T(8,128)(2,1)} %slice_bitcast_fusion.2), channel_id=1, source_target_pairs={{24,0},{26,2},{28,4},{30,6},{0,8},{2,10},{4,12},{6,14},{8,16},{10,... | collective-permute-start | bytes 1966088 | tf_op jit(solution)/shard_map/cond/branch_2_fun/ppermute | solution.py:30
  13.4 125.3 %collective-permute-start.19 = (bf16[512,5120]{1,0:T(8,128)(2,1)}, bf16[512,5120]{1,0:T(8,128)(2,1)}, u32[]{:S(2)}, u32[]{:S(2)}) collective-permute-start(bf16[512,5120]{1,0:T(8,128)(2,1)} %slice.86), channel_id=1, source_target_pairs={{24,0},{26,2},{28,4},{30,6},{0,8},{2,10},{4,12},{6,14},{8,16},{10,... | collective-permute-start | bytes 15728648 | tf_op jit(solution)/shard_map/cond/branch_2_fun/ppermute | solution.py:30
  21.8 285.4 %collective-permute-start.20 = (bf16[768,5120]{1,0:T(8,128)(2,1)}, bf16[768,5120]{1,0:T(8,128)(2,1)}, u32[]{:S(2)}, u32[]{:S(2)}) collective-permute-start(bf16[768,5120]{1,0:T(8,128)(2,1)} %slice.87), channel_id=1, source_target_pairs={{24,0},{26,2},{28,4},{30,6},{0,8},{2,10},{4,12},{6,14},{8,16},{10,... | collective-permute-start | bytes 23592968 | tf_op jit(solution)/shard_map/cond/branch_2_fun/ppermute | solution.py:30
  23.3 316.3 %collective-permute-start.22 = (f32[1]{0:T(128)}, f32[1]{0:T(128)}, u32[]{:S(2)}, u32[]{:S(2)}) collective-permute-start(f32[1]{0:T(128)} %get-tuple-element.93), channel_id=1, source_target_pairs={{24,0},{26,2},{28,4},{30,6},{0,8},{2,10},{4,12},{6,14},{8,16},{10,... | collective-permute-start | bytes 20 | tf_op jit(solution)/shard_map/cond/branch_2_fun/ppermute | solution.py:30
  23.6 9.5 %copy-start.6 = (bf16[256,1536]{1,0:T(8,128)(2,1)S(1)}, bf16[256,1536]{1,0:T(8,128)(2,1)}, u32[]{:S(2)}) copy-start(bf16[256,1536]{1,0:T(8,128)(2,1)} %get-tuple-element.162) | copy-start | bytes 2359300
  33.1 7.1 %copy-start.2 = (bf16[1536,5120]{1,0:T(8,128)(2,1)}, bf16[1536,5120]{1,0:T(8,128)(2,1)S(1)}, u32[]{:S(2)}) copy-start(bf16[1536,5120]{1,0:T(8,128)(2,1)S(1)} %divide_convert_fusion.2) | copy-start | bytes 47185924
  50.8 284.5 %collective-permute-start.21 = (bf16[128,5120]{1,0:T(8,128)(2,1)}, bf16[128,5120]{1,0:T(8,128)(2,1)}, u32[]{:S(2)}, u32[]{:S(2)}) collective-permute-start(bf16[128,5120]{1,0:T(8,128)(2,1)} %slice.88), channel_id=1, source_target_pairs={{24,0},{26,2},{28,4},{30,6},{0,8},{2,10},{4,12},{6,14},{8,16},{10,... | collective-permute-start | bytes 3932168 | tf_op jit(solution)/shard_map/cond/branch_2_fun/ppermute | solution.py:30
  53.8 29.2 %collective-permute-start.16 = (bf16[128,5120]{1,0:T(8,128)(2,1)}, bf16[128,5120]{1,0:T(8,128)(2,1)}, u32[]{:S(2)}, u32[]{:S(2)}) collective-permute-start(bf16[128,5120]{1,0:T(8,128)(2,1)} %fusion.17), channel_id=1, source_target_pairs={{1,0},{0,1},{3,2},{2,3},{5,4},{4,5},{7,6},{6,7},{9,8},{8,9},{11,10... | collective-permute-start | bytes 3932168 | tf_op jit(solution)/shard_map/cond/branch_2_fun/ppermute | solution.py:30
  83.0 264.8 %collective-permute-start.23 = (bf16[64,5120]{1,0:T(8,128)(2,1)}, bf16[64,5120]{1,0:T(8,128)(2,1)S(1)}, u32[]{:S(2)}, u32[]{:S(2)}) collective-permute-start(bf16[64,5120]{1,0:T(8,128)(2,1)} %slice.91), channel_id=1, source_target_pairs={{24,0},{26,2},{28,4},{30,6},{0,8},{2,10},{4,12},{6,14},{8,16},{10,... | collective-permute-start | bytes 1966088 | tf_op jit(solution)/shard_map/cond/branch_2_fun/ppermute | solution.py:30
  88.6 218.5 %slice-start.8 = ((s8[15728640]{0:T(1024)(128)(4,1)}), s8[4194304]{0:T(1024)(128)(4,1)S(1)}, s32[]{:S(2)}) async-start(s8[15728640]{0:T(1024)(128)(4,1)} %bitcast.162), calls=%async_computation.8 | async-start | bytes 8388608
  90.5 216.7 %slice-start.9 = ((s8[15728640]{0:T(1024)(128)(4,1)}), s8[4194304]{0:T(1024)(128)(4,1)S(1)}, s32[]{:S(2)}) async-start(s8[15728640]{0:T(1024)(128)(4,1)} %bitcast.162), calls=%async_computation.9 | async-start | bytes 8388608
  90.5 216.7 %slice-start.10 = ((s8[15728640]{0:T(1024)(128)(4,1)}), s8[4194304]{0:T(1024)(128)(4,1)S(1)}, s32[]{:S(2)}) async-start(s8[15728640]{0:T(1024)(128)(4,1)} %bitcast.162), calls=%async_computation.10 | async-start | bytes 8388608
  90.5 216.7 %slice-start.11 = ((s8[15728640]{0:T(1024)(128)(4,1)}), s8[3145728]{0:T(1024)(128)(4,1)S(1)}, s32[]{:S(2)}) async-start(s8[15728640]{0:T(1024)(128)(4,1)} %bitcast.162), calls=%async_computation.11 | async-start | bytes 6291456

commit v2 on v1

--- a/solution.py
+++ b/solution.py
@@ -14,14 +14,14 @@
 LEARN = 0.001
 
 
-PIECES = ((23, 1), (0, 8), (8, 12), (20, 2), (22, 1))
+PIECES = ((44, 2), (0, 16), (16, 24), (40, 4), (46, 2))
+LONG_PIECES = ((44, 3), (0, 16), (16, 24), (40, 4), (47, 1))
 
 
-def pieces_of(rows):
-    if rows % (24 * 16):
-        return ((0, rows),)
-    unit = rows // 24
-    return tuple((start * unit, size * unit) for start, size in PIECES)
+def pieces_of(rows, distance):
+    unit = rows // 48
+    pieces = PIECES if distance == 1 else LONG_PIECES
+    return tuple((start * unit, size * unit) for start, size in pieces)
 
 
 def from_behind(block, axis, distance):
@@ -30,17 +30,18 @@
     return lax.ppermute(block, axis, route)
 
 
-def mix_body(ctx_ref, cot_ref, own_ref, peer_ref, *rest):
+def mix_body(tile, ctx_ref, cot_ref, own_ref, peer_ref, *rest):
     out_ref = rest[-1]
     width = out_ref.shape[1]
-    tile = 512 if width % 512 == 0 else width
+    first = pl.program_id(1) * width
 
     @pl.loop(0, width // tile)
     def _(j):
-        cols = pl.ds(pl.multiple_of(j * tile, tile), tile)
+        here = pl.ds(pl.multiple_of(j * tile, tile), tile)
+        cols = pl.ds(pl.multiple_of(first + j * tile, tile), tile)
         grad = jnp.dot(ctx_ref[...], cot_ref[:, cols], preferred_element_type=jnp.float32)
-        both = own_ref[:, cols].astype(jnp.float32) + peer_ref[:, cols].astype(jnp.float32)
-        out_ref[:, cols] = (0.5 * both - LEARN * grad).astype(out_ref.dtype)
+        both = own_ref[:, here].astype(jnp.float32) + peer_ref[:, here].astype(jnp.float32)
+        out_ref[:, here] = (0.5 * both - LEARN * grad).astype(out_ref.dtype)
 
 
 def mix_rows(start, size, ctx_t, cot, own, peer, so_far):
@@ -48,11 +49,13 @@
     tokens = cot.shape[0]
     block = next(b for b in (128, 64, 32, 16, 8, size) if size % b == 0 and start % b == 0)
     first = start // block
+    wide = width // 4 if size <= block and width % (4 * 128) == 0 else width
+    tile = next(t for t in (640, 512, 256, 128, wide) if wide % t == 0)
     in_specs = [
-        pl.BlockSpec((block, tokens), lambda i: (first + i, 0)),
-        pl.BlockSpec((tokens, width), lambda i: (0, 0)),
-        pl.BlockSpec((block, width), lambda i: (first + i, 0)),
-        pl.BlockSpec((block, width), lambda i: (i, 0)),
+        pl.BlockSpec((block, tokens), lambda i, j: (first + i, 0)),
+        pl.BlockSpec((tokens, width), lambda i, j: (0, 0)),
+        pl.BlockSpec((block, wide), lambda i, j: (first + i, j)),
+        pl.BlockSpec((block, wide), lambda i, j: (i, j)),
     ]
     operands = [ctx_t, cot, own, peer]
     aliases = {}
@@ -61,10 +64,10 @@
         operands.append(so_far)
         aliases = {4: 0}
     return pl.pallas_call(
-        mix_body,
-        grid=(size // block,),
+        partial(mix_body, tile),
+        grid=(size // block, width // wide),
         in_specs=in_specs,
-        out_specs=pl.BlockSpec((block, width), lambda i: (first + i, 0)),
+        out_specs=pl.BlockSpec((block, wide), lambda i, j: (first + i, j)),
         out_shape=jax.ShapeDtypeStruct((rows, width), own.dtype),
         input_output_aliases=aliases,
         compiler_params=pltpu.CompilerParams(vmem_limit_bytes=24 * 2**20),
@@ -82,7 +85,7 @@
 def step_at(bits, context, residual, cotangent, numer, weight):
     distance = 1 << bits
     own_numer = numer[0]
-    pieces = pieces_of(own_numer.shape[0])
+    pieces = pieces_of(own_numer.shape[0], distance)
     peer_weight = from_behind(weight, "rep", distance)
     arrived = []
     source = own_numer
@@ -123,8 +126,8 @@
         if numer_next is not None:
             numer_next, peer = lax.optimization_barrier((numer_next, peer))
         numer_next = mix_rows(start, size, ctx_t, cot, own_numer, peer, numer_next)
-    numer_next, base, peer_weight = lax.optimization_barrier((numer_next, base, peer_weight))
     weight_next = 0.5 * (weight + peer_weight)
+    numer_next, base, weight_next = lax.optimization_barrier((numer_next, base, weight_next))
     last = (base + 0.5 * arrived[-1].astype(jnp.float32)).astype(jnp.bfloat16)
     numer_next = lax.dynamic_update_slice(numer_next, last, (pieces[-1][0], 0))
     return output, grad_ctx, numer_next[None], weight_next

time: 351 us -> 384 us (1.094)
  waiting for transfers between devices: 242 us -> 275 us
    ppermute x8, waiting for transfers between devices: 242 us -> 275 us  [from_behind(): return lax.ppermute(block, axis, route)]
  transfers between devices with their start and end apart: 8 -> 8, of which waited for: 5 -> 2; matrix products, arithmetic and copies ran while one was open for 16% -> 15% of each run, Pallas kernels for 10% -> 9%
where the time goes in v2:
time: 384 us
  waiting for transfers between devices  275 us (72%)
  Pallas kernels  36.3 us (9%)
  local copies, waits for them, and re-layouts  24.9 us (6%)
  matrix products  18.1 us (5%)
  other arithmetic  15.5 us (4%)
  starting transfers between devices  9.93 us (3%)
    ppermute x8, waiting for transfers between devices, from_behind(): return lax.ppermute(block, axis, route)  275 us
    pallas_call x4, Pallas kernels, mix_rows(): pl.pallas_call(partial(mix_body, tile), grid=(size // block, width // wid...  36.3 us
    slice x5, local copies, waits for them, and re-layouts, step_at(): piece = lax.slice_in_dim(source, start, start + size, axis=0)  18.4 us
    ppermute x8, starting transfers between devices, from_behind(): return lax.ppermute(block, axis, route)  9.93 us
    convert_element_type x1, other arithmetic, step_at(): params = (own_numer.astype(jnp.float32) / weight[0]).astype(jnp.bfloat16)  9.52 us
    dot_general x1, matrix products, step_at(): lax.dot_general(cot, params, (((1,), (1,)), ((), ())), preferred_element_...  8.65 us
  transfers between devices with their start and end apart: 8, of which 2 were waited for; matrix products, arithmetic and copies ran while one was open for 15% of the time, Pallas kernels for 9%

profile of v2, /device:TPU:0, one launch (start us, length us, event | category | flops | bytes accessed | tf_op | source)
XLA Modules:
  0.0 383.6 jit_solution(8554729521181600893)
XLA Ops:
  1.3 381.1 %conditional.3 = (bf16[128,5120]{1,0:T(8,128)(2,1)}, bf16[256,1536]{1,0:T(8,128)(2,1)}, bf16[1,1536,5120]{2,1,0:T(8,128)(2,1)}, f32[1]{0:T(128)}) conditional(s32[]{:T(128)} %clamp.3, (bf16[128,5120]{1,0:T(8,128)(2,1)}, bf16[1,1536,5120]{2,1,0:T(8,128)(2,1)}, f32[1]{0:T(128)}, bf16[256,1536]{1,0:T(8,128)(2,1)}, ...), branch_computations={%region_0.1_spmd, %region_1.2_spmd, %region_2.3_spmd, %region_3.4_... | conditional | flops 12109086720 | bytes 362824544
  1.6 3.0 collective-permute-start.17
  4.6 2.2 slice_bitcast_fusion.2
  6.8 1.6 collective-permute-start.18
  8.4 5.2 %slice.86 = bf16[512,5120]{1,0:T(8,128)(2,1)} slice(bf16[1536,5120]{1,0:T(8,128)(2,1)} %bitcast.156), slice={[0:512], [0:5120]} | slice | bytes 10485760 | tf_op jit(solution)/shard_map/cond/branch_2_fun/slice | solution.py:93
  13.6 1.6 collective-permute-start.19
  15.2 6.8 %slice.87 = bf16[768,5120]{1,0:T(8,128)(2,1)} slice(bf16[1536,5120]{1,0:T(8,128)(2,1)} %bitcast.157), slice={[512:1280], [0:5120]} | slice | bytes 15728640 | tf_op jit(solution)/shard_map/cond/branch_2_fun/slice | solution.py:93
  22.0 1.6 collective-permute-start.20
  23.6 0.2 collective-permute-start.22
  23.8 0.0 copy-start.6
  23.8 9.5 %divide_convert_fusion.2 = bf16[1536,5120]{1,0:T(8,128)(2,1)S(1)} fusion(f32[]{:T(128)} %bitcast.21, bf16[1,1536,5120]{2,1,0:T(8,128)(2,1)} %get-tuple-element.92), kind=kLoop, calls=%fused_computation.30 | loop fusion | flops 23592960 | bytes 31457284 | tf_op jit(solution)/shard_map/cond/branch_2_fun/convert_element_type | solution.py:107
  33.3 0.0 copy-start.1
  33.3 0.0 copy-done.6
  33.3 7.1 %fusion.33 = f32[5120,256]{0,1:T(8,128)} fusion(bf16[256,1536]{1,0:T(8,128)(2,1)S(1)} %copy-done.6, bf16[1536,5120]{1,0:T(8,128)(2,1)S(1)} %divide_convert_fusion.2), kind=kOutput, calls=%fused_computation.65 | convolution fusion | flops 4026531840 | bytes 21757952 | tf_op jit(solution)/shard_map/cond/branch_2_fun/dot_general | solution.py:108
  40.4 0.0 copy-done.1
  40.5 0.3 copy.32
  40.7 2.5 slice.88
  43.2 1.7 slice.91
  44.9 0.3 broadcast.65
  45.2 1.5 constant_dynamic-update-slice_fusion.5
  46.7 3.0 fusion.17
  49.6 263.6 %collective-permute-done.22 = f32[1]{0:T(128)} collective-permute-done((f32[1]{0:T(128)}, f32[1]{0:T(128)}, u32[]{:S(2)}, u32[]{:S(2)}) %collective-permute-start.22) | collective-permute-done | bytes 36 | tf_op jit(solution)/shard_map/cond/branch_2_fun/ppermute | solution.py:30
  313.2 0.0 collective-permute-start.21
  314.5 0.0 collective-permute-done.17
  314.5 1.3 collective-permute-start.23
  315.8 1.5 constant_dynamic-update-slice_fusion.4.cot_ref
  317.3 0.0 collective-permute-done.18.peer_ref
  317.3 0.6 collective-permute-start.16
  317.9 6.3 %branch_2_fun.4.rest_0_ = bf16[1536,5120]{1,0:T(8,128)(2,1)} custom-call(bf16[1536,256]{1,0:T(8,128)(2,1)S(1)} %bitcast.126, bf16[256,5120]{1,0:T(8,128)(2,1)S(1)} %constant_dynamic-update-slice_fusion.4.cot_ref, bf16[1536,5120]{1,0:T(8,128)(2,1)} %bitcast.160, bf16[96,5120]{1,0:T(8,128)(2,1)} %collective-permute-done.18.peer_ref), custom_call_target="tpu_custom_call" | custom-call | flops 251658240 | bytes 2949120 | tf_op jit(solution)/shard_map/cond/branch_2_fun/pallas_call | solution.py:66
  324.2 2.4 fusion.15
  326.6 8.6 %fusion.32 = bf16[256,1536]{1,0:T(8,128)(2,1)} fusion(bf16[256,5120]{1,0:T(8,128)(2,1)S(1)} %constant_dynamic-update-slice_fusion.4.cot_ref, bf16[1536,5120]{1,0:T(8,128)(2,1)} %copy-done.1), kind=kOutput, calls=%fused_computation.64 | convolution fusion | flops 4026531840 | bytes 19136512 | tf_op jit(solution)/shard_map/cond/branch_2_fun/dot_general | solution.py:118
  335.2 11.2 %collective-permute-done.16 = bf16[128,5120]{1,0:T(8,128)(2,1)} collective-permute-done((bf16[128,5120]{1,0:T(8,128)(2,1)}, bf16[128,5120]{1,0:T(8,128)(2,1)}, u32[]{:S(2)}, u32[]{:S(2)}) %collective-permute-start.16) | collective-permute-done | bytes 1310752 | tf_op jit(solution)/shard_map/cond/branch_2_fun/ppermute | solution.py:30
  346.4 0.0 slice-start.8
  346.4 4.2 %fusion.16 = bf16[128,5120]{1,0:T(8,128)(2,1)} fusion(bf16[128,5120]{1,0:T(8,128)(2,1)} %collective-permute-done.16, f32[5120,256]{0,1:T(8,128)} %fusion.33, s32[]{:T(128)S(6)} %select_n.40, bf16[128,5120]{1,0:T(8,128)(2,1)} %get-tuple-element.91), kind=kLoop, calls=%fused_computation.35 | loop fusion | flops 3276800 | bytes 6553604 | tf_op jit(solution)/shard_map/cond/branch_2_fun/add | solution.py:115
  350.6 0.0 slice-start.9
  350.6 0.0 collective-permute-done.19.peer_ref
  350.6 12.2 %branch_2_fun.5.rest_0_ = bf16[1536,5120]{1,0:T(8,128)(2,1)} custom-call(bf16[1536,256]{1,0:T(8,128)(2,1)S(1)} %bitcast.128, bf16[256,5120]{1,0:T(8,128)(2,1)S(1)} %constant_dynamic-update-slice_fusion.4.cot_ref, bf16[1536,5120]{1,0:T(8,128)(2,1)} %bitcast.161, bf16[512,5120]{1,0:T(8,128)(2,1)} %collective-permute-done.19.peer_ref, ...), custom_call_target="tpu_custom_call", output_to_operand_aliasing={{}: (4, {})} | custom-call | flops 1342177280 | bytes 15728640 | tf_op jit(solution)/shard_map/cond/branch_2_fun/pallas_call | solution.py:66
  362.8 0.0 collective-permute-done.20.peer_ref
  362.8 0.0 slice-done.8
  362.9 0.0 slice-done.9
  362.9 0.0 slice-done.10
  362.9 0.0 slice-done.11
  362.9 13.3 %branch_2_fun.6.rest_0_ = bf16[1536,5120]{1,0:T(8,128)(2,1)} custom-call(bf16[1536,256]{1,0:T(8,128)(2,1)S(1)} %bitcast.129, bf16[256,5120]{1,0:T(8,128)(2,1)S(1)} %constant_dynamic-update-slice_fusion.4.cot_ref, bf16[1536,5120]{1,0:T(8,128)(2,1)S(1)} %bitcast.164, ...), custom_call_target="tpu_custom_call", output_to_operand_aliasing={{}: (4, {})} | custom-call | flops 2013265920 | bytes 23592960 | tf_op jit(solution)/shard_map/cond/branch_2_fun/pallas_call | solution.py:66
  376.2 0.0 collective-permute-done.21.peer_ref
  376.2 4.4 %branch_2_fun.7 = bf16[1536,5120]{1,0:T(8,128)(2,1)} custom-call(bf16[1536,256]{1,0:T(8,128)(2,1)S(1)} %bitcast.130, bf16[256,5120]{1,0:T(8,128)(2,1)S(1)} %constant_dynamic-update-slice_fusion.4.cot_ref, bf16[1536,5120]{1,0:T(8,128)(2,1)S(1)} %bitcast.165, bf16[128,5120]{1,0:T(8,128)(2,1)} %collective-permute-done.21.peer_ref, ...), custom_call_target="tpu_custom_call", output_to_operand_aliasing={{}: (4, {})} | custom-call | flops 335544320 | bytes 3932160 | tf_op jit(solution)/shard_map/cond/branch_2_fun/pallas_call | solution.py:66
  380.7 0.0 collective-permute-done.23
  380.7 0.0 copy-done.9
  380.7 1.8 fusion.19
  (4 shorter events, 0.0 us)
Async XLA Ops:
  1.6 312.9 %collective-permute-start.17 = (bf16[128,5120]{1,0:T(8,128)(2,1)}, bf16[128,5120]{1,0:T(8,128)(2,1)}, u32[]{:S(2)}, u32[]{:S(2)}) collective-permute-start(bf16[128,5120]{1,0:T(8,128)(2,1)} %get-tuple-element.95), channel_id=1, source_target_pairs={{1,0},{0,1},{3,2},{2,3},{5,4},{4,5},{7,6},{6,7},{9,8},{8,9},{11,10... | collective-permute-start | bytes 3932168 | tf_op jit(solution)/shard_map/cond/branch_2_fun/ppermute | solution.py:30
  6.8 310.5 %collective-permute-start.18 = (bf16[96,5120]{1,0:T(8,128)(2,1)}, bf16[96,5120]{1,0:T(8,128)(2,1)}, u32[]{:S(2)}, u32[]{:S(2)}) collective-permute-start(bf16[96,5120]{1,0:T(8,128)(2,1)} %slice_bitcast_fusion.2), channel_id=1, source_target_pairs={{24,0},{26,2},{28,4},{30,6},{0,8},{2,10},{4,12},{6,14},{8,16},{10,... | collective-permute-start | bytes 2949128 | tf_op jit(solution)/shard_map/cond/branch_2_fun/ppermute | solution.py:30
  13.6 337.0 %collective-permute-start.19 = (bf16[512,5120]{1,0:T(8,128)(2,1)}, bf16[512,5120]{1,0:T(8,128)(2,1)}, u32[]{:S(2)}, u32[]{:S(2)}) collective-permute-start(bf16[512,5120]{1,0:T(8,128)(2,1)} %slice.86), channel_id=1, source_target_pairs={{24,0},{26,2},{28,4},{30,6},{0,8},{2,10},{4,12},{6,14},{8,16},{10,... | collective-permute-start | bytes 15728648 | tf_op jit(solution)/shard_map/cond/branch_2_fun/ppermute | solution.py:30
  22.0 340.9 %collective-permute-start.20 = (bf16[768,5120]{1,0:T(8,128)(2,1)}, bf16[768,5120]{1,0:T(8,128)(2,1)}, u32[]{:S(2)}, u32[]{:S(2)}) collective-permute-start(bf16[768,5120]{1,0:T(8,128)(2,1)} %slice.87), channel_id=1, source_target_pairs={{24,0},{26,2},{28,4},{30,6},{0,8},{2,10},{4,12},{6,14},{8,16},{10,... | collective-permute-start | bytes 23592968 | tf_op jit(solution)/shard_map/cond/branch_2_fun/ppermute | solution.py:30
  23.6 289.6 %collective-permute-start.22 = (f32[1]{0:T(128)}, f32[1]{0:T(128)}, u32[]{:S(2)}, u32[]{:S(2)}) collective-permute-start(f32[1]{0:T(128)} %get-tuple-element.93), channel_id=1, source_target_pairs={{24,0},{26,2},{28,4},{30,6},{0,8},{2,10},{4,12},{6,14},{8,16},{10,... | collective-permute-start | bytes 20 | tf_op jit(solution)/shard_map/cond/branch_2_fun/ppermute | solution.py:30
  23.8 9.5 %copy-start.6 = (bf16[256,1536]{1,0:T(8,128)(2,1)S(1)}, bf16[256,1536]{1,0:T(8,128)(2,1)}, u32[]{:S(2)}) copy-start(bf16[256,1536]{1,0:T(8,128)(2,1)} %get-tuple-element.162) | copy-start | bytes 2359300
  33.3 7.1 %copy-start.1 = (bf16[1536,5120]{1,0:T(8,128)(2,1)}, bf16[1536,5120]{1,0:T(8,128)(2,1)S(1)}, u32[]{:S(2)}) copy-start(bf16[1536,5120]{1,0:T(8,128)(2,1)S(1)} %divide_convert_fusion.2) | copy-start | bytes 47185924
  313.2 63.0 %collective-permute-start.21 = (bf16[128,5120]{1,0:T(8,128)(2,1)}, bf16[128,5120]{1,0:T(8,128)(2,1)}, u32[]{:S(2)}, u32[]{:S(2)}) collective-permute-start(bf16[128,5120]{1,0:T(8,128)(2,1)} %slice.88), channel_id=1, source_target_pairs={{24,0},{26,2},{28,4},{30,6},{0,8},{2,10},{4,12},{6,14},{8,16},{10,... | collective-permute-start | bytes 3932168 | tf_op jit(solution)/shard_map/cond/branch_2_fun/ppermute | solution.py:30
  314.5 66.2 %collective-permute-start.23 = (bf16[32,5120]{1,0:T(8,128)(2,1)}, bf16[32,5120]{1,0:T(8,128)(2,1)}, u32[]{:S(2)}, u32[]{:S(2)}) collective-permute-start(bf16[32,5120]{1,0:T(8,128)(2,1)} %slice.91), channel_id=1, source_target_pairs={{24,0},{26,2},{28,4},{30,6},{0,8},{2,10},{4,12},{6,14},{8,16},{10,... | collective-permute-start | bytes 983048 | tf_op jit(solution)/shard_map/cond/branch_2_fun/ppermute | solution.py:30
  317.3 29.1 %collective-permute-start.16 = (bf16[128,5120]{1,0:T(8,128)(2,1)}, bf16[128,5120]{1,0:T(8,128)(2,1)}, u32[]{:S(2)}, u32[]{:S(2)}) collective-permute-start(bf16[128,5120]{1,0:T(8,128)(2,1)} %fusion.17), channel_id=1, source_target_pairs={{1,0},{0,1},{3,2},{2,3},{5,4},{4,5},{7,6},{6,7},{9,8},{8,9},{11,10... | collective-permute-start | bytes 3932168 | tf_op jit(solution)/shard_map/cond/branch_2_fun/ppermute | solution.py:30
  346.4 16.4 %slice-start.8 = ((s8[15728640]{0:T(1024)(128)(4,1)}), s8[4194304]{0:T(1024)(128)(4,1)S(1)}, s32[]{:S(2)}) async-start(s8[15728640]{0:T(1024)(128)(4,1)} %bitcast.162), calls=%async_computation.8 | async-start | bytes 8388608
  350.6 12.3 %slice-start.9 = ((s8[15728640]{0:T(1024)(128)(4,1)}), s8[4194304]{0:T(1024)(128)(4,1)S(1)}, s32[]{:S(2)}) async-start(s8[15728640]{0:T(1024)(128)(4,1)} %bitcast.162), calls=%async_computation.9 | async-start | bytes 8388608
  350.6 12.3 %slice-start.10 = ((s8[15728640]{0:T(1024)(128)(4,1)}), s8[4194304]{0:T(1024)(128)(4,1)S(1)}, s32[]{:S(2)}) async-start(s8[15728640]{0:T(1024)(128)(4,1)} %bitcast.162), calls=%async_computation.10 | async-start | bytes 8388608
  350.6 12.3 %slice-start.11 = ((s8[15728640]{0:T(1024)(128)(4,1)}), s8[3145728]{0:T(1024)(128)(4,1)S(1)}, s32[]{:S(2)}) async-start(s8[15728640]{0:T(1024)(128)(4,1)} %bitcast.162), calls=%async_computation.11 | async-start | bytes 6291456
  376.2 4.4 %copy-start.9 = (f32[32,5120]{1,0:T(8,128)S(1)}, f32[32,5120]{1,0:T(8,128)}, u32[]{:S(2)}) copy-start(f32[32,5120]{1,0:T(8,128)} %fusion.15) | copy-start | bytes 1966084

commit v3 on v2

--- a/solution.py
+++ b/solution.py
@@ -15,13 +15,11 @@
 
 
 PIECES = ((44, 2), (0, 16), (16, 24), (40, 4), (46, 2))
-LONG_PIECES = ((44, 3), (0, 16), (16, 24), (40, 4), (47, 1))
 
 
-def pieces_of(rows, distance):
+def pieces_of(rows):
     unit = rows // 48
-    pieces = PIECES if distance == 1 else LONG_PIECES
-    return tuple((start * unit, size * unit) for start, size in pieces)
+    return tuple((start * unit, size * unit) for start, size in PIECES)
 
 
 def from_behind(block, axis, distance):
@@ -82,15 +80,15 @@
     return 0.5 * own[start : start + size].astype(jnp.float32) - LEARN * grad
 
 
-def step_at(bits, context, residual, cotangent, numer, weight):
+def step_at(bits, context, residual, cotangent, numer, weight, head):
     distance = 1 << bits
     own_numer = numer[0]
-    pieces = pieces_of(own_numer.shape[0], distance)
+    pieces = pieces_of(own_numer.shape[0])
     peer_weight = from_behind(weight, "rep", distance)
     arrived = []
     source = own_numer
-    for start, size in pieces:
-        piece = lax.slice_in_dim(source, start, start + size, axis=0)
+    for n, (start, size) in enumerate(pieces):
+        piece = lax.slice_in_dim(source, start, start + size, axis=0) if n else head
         source, piece = lax.optimization_barrier((source, piece))
         arrived.append(from_behind(piece, "rep", distance))
 
@@ -140,7 +138,10 @@
 def on_device(context, residual, cotangent, numer, weight, step):
     exponent = jnp.remainder(step[0], jnp.int32(PEER_BITS + 1))
     branches = [partial(branch, bits) for bits in range(PEER_BITS + 1)]
-    return lax.switch(exponent, branches, context, residual, cotangent, numer, weight)
+    start, size = pieces_of(numer.shape[1])[0]
+    head = lax.slice_in_dim(numer[0], start, start + size, axis=0)
+    head = lax.optimization_barrier(head)
+    return lax.switch(exponent, branches, context, residual, cotangent, numer, weight, head)
 
 
 def solution(mesh):

time: 384 us -> 379 us (0.987)
  waiting for transfers between devices: 275 us -> 271 us
  transfers between devices with their start and end apart: 8 -> 8, of which waited for: 2 -> 2; matrix products, arithmetic and copies ran while one was open for 15% -> 14% of each run, Pallas kernels for 9% -> 9%
where the time goes in v3:
time: 379 us; the launch traced here: 378 us
  waiting for transfers between devices  271 us (72%)
  Pallas kernels  33.9 us (9%)
  local copies, waits for them, and re-layouts  26.4 us (7%)
  matrix products  17.2 us (5%)
  other arithmetic  15.6 us (4%)
  starting transfers between devices  9.86 us (3%)
    ppermute x8, waiting for transfers between devices, from_behind(): return lax.ppermute(block, axis, route)  271 us
    pallas_call x4, Pallas kernels, mix_rows(): pl.pallas_call(partial(mix_body, tile), grid=(size // block, width // wid...  33.9 us
    slice x4, local copies, waits for them, and re-layouts, step_at(): piece = lax.slice_in_dim(source, start, start + size, axis=0) if n else head  16.5 us
    ppermute x8, starting transfers between devices, from_behind(): return lax.ppermute(block, axis, route)  9.86 us
    convert_element_type x1, other arithmetic, step_at(): params = (own_numer.astype(jnp.float32) / weight[0]).astype(jnp.bfloat16)  9.52 us
    dot_general x1, matrix products, step_at(): lax.dot_general(cot, params, (((1,), (1,)), ((), ())), preferred_element_...  8.65 us
  transfers between devices with their start and end apart: 8, of which 2 were waited for; matrix products, arithmetic and copies ran while one was open for 14% of the time, Pallas kernels for 9%

profile of v3, /device:TPU:0, one launch (start us, length us, event | category | flops | bytes accessed | tf_op | source)
XLA Modules:
  0.0 377.9 jit_solution(10688345525873061519)
XLA Ops:
  1.3 2.0 slice_bitcast_fusion
  3.3 373.4 %conditional.3 = (bf16[128,5120]{1,0:T(8,128)(2,1)}, bf16[256,1536]{1,0:T(8,128)(2,1)}, bf16[1,1536,5120]{2,1,0:T(8,128)(2,1)}, f32[1]{0:T(128)}) conditional(s32[]{:T(128)} %clamp.3, (bf16[128,5120]{1,0:T(8,128)(2,1)}, bf16[1,1536,5120]{2,1,0:T(8,128)(2,1)}, f32[1]{0:T(128)}, bf16[256,1536]{1,0:T(8,128)(2,1)}, ...), branch_computations={%region_0.1_spmd, %region_1.2_spmd, %region_2.3_spmd, %region_3.4_... | conditional | flops 12109086720 | bytes 360219456
  3.3 3.0 collective-permute-start.17
  6.3 1.6 collective-permute-start.18
  7.8 5.2 %slice.68 = bf16[512,5120]{1,0:T(8,128)(2,1)} slice(bf16[1536,5120]{1,0:T(8,128)(2,1)} %bitcast.150), slice={[0:512], [0:5120]} | slice | bytes 10485760 | tf_op jit(solution)/shard_map/cond/branch_2_fun/slice | solution.py:91
  13.1 1.6 collective-permute-start.19
  14.7 6.8 %slice.69 = bf16[768,5120]{1,0:T(8,128)(2,1)} slice(bf16[1536,5120]{1,0:T(8,128)(2,1)} %bitcast.151), slice={[512:1280], [0:5120]} | slice | bytes 15728640 | tf_op jit(solution)/shard_map/cond/branch_2_fun/slice | solution.py:91
  21.5 1.6 collective-permute-start.20
  23.0 0.2 collective-permute-start.22
  23.3 0.0 copy-start.6
  23.3 9.5 %divide_convert_fusion.2 = bf16[1536,5120]{1,0:T(8,128)(2,1)S(1)} fusion(f32[]{:T(128)} %bitcast.19, bf16[1,1536,5120]{2,1,0:T(8,128)(2,1)} %get-tuple-element.102), kind=kLoop, calls=%fused_computation.28 | loop fusion | flops 23592960 | bytes 31457284 | tf_op jit(solution)/shard_map/cond/branch_2_fun/convert_element_type | solution.py:105
  32.8 0.0 copy-start.2
  32.8 0.0 copy-done.6
  32.8 6.7 %fusion.33 = f32[5120,256]{0,1:T(8,128)} fusion(bf16[256,1536]{1,0:T(8,128)(2,1)S(1)} %copy-done.6, bf16[1536,5120]{1,0:T(8,128)(2,1)S(1)} %divide_convert_fusion.2), kind=kOutput, calls=%fused_computation.62 | convolution fusion | flops 4026531840 | bytes 21757952 | tf_op jit(solution)/shard_map/cond/branch_2_fun/dot_general | solution.py:106
  39.5 0.3 copy-done.2
  39.9 0.3 broadcast.65
  40.1 1.5 constant_dynamic-update-slice_fusion.5
  41.6 3.0 fusion.17
  44.6 1.4 copy.32
  46.0 2.5 slice.70
  48.5 2.0 slice.73
  50.4 255.2 %collective-permute-done.22 = f32[1]{0:T(128)} collective-permute-done((f32[1]{0:T(128)}, f32[1]{0:T(128)}, u32[]{:S(2)}, u32[]{:S(2)}) %collective-permute-start.22) | collective-permute-done | bytes 36 | tf_op jit(solution)/shard_map/cond/branch_2_fun/ppermute | solution.py:28
  305.6 0.0 collective-permute-start.21
  306.9 0.0 collective-permute-done.17
  306.9 1.3 collective-permute-start.23
  308.2 1.5 constant_dynamic-update-slice_fusion.4.cot_ref
  309.7 0.0 collective-permute-done.18.peer_ref
  309.7 0.6 collective-permute-start.16
  310.3 4.1 %branch_2_fun.4.rest_0_ = bf16[1536,5120]{1,0:T(8,128)(2,1)} custom-call(bf16[1536,256]{1,0:T(8,128)(2,1)S(1)} %bitcast.120, bf16[256,5120]{1,0:T(8,128)(2,1)S(1)} %constant_dynamic-update-slice_fusion.4.cot_ref, bf16[1536,5120]{1,0:T(8,128)(2,1)} %bitcast.154, bf16[64,5120]{1,0:T(8,128)(2,1)} %collective-permute-done.18.peer_ref), custom_call_target="tpu_custom_call" | custom-call | flops 167772160 | bytes 1966080 | tf_op jit(solution)/shard_map/cond/branch_2_fun/pallas_call | solution.py:64
  314.4 8.7 %fusion.32 = bf16[256,1536]{1,0:T(8,128)(2,1)} fusion(bf16[256,5120]{1,0:T(8,128)(2,1)S(1)} %constant_dynamic-update-slice_fusion.4.cot_ref, bf16[1536,5120]{1,0:T(8,128)(2,1)} %copy-done.2), kind=kOutput, calls=%fused_computation.61 | convolution fusion | flops 4026531840 | bytes 19136512 | tf_op jit(solution)/shard_map/cond/branch_2_fun/dot_general | solution.py:116
  323.1 15.7 %collective-permute-done.16 = bf16[128,5120]{1,0:T(8,128)(2,1)} collective-permute-done((bf16[128,5120]{1,0:T(8,128)(2,1)}, bf16[128,5120]{1,0:T(8,128)(2,1)}, u32[]{:S(2)}, u32[]{:S(2)}) %collective-permute-start.16) | collective-permute-done | bytes 1310752 | tf_op jit(solution)/shard_map/cond/branch_2_fun/ppermute | solution.py:28
  338.8 4.0 %fusion.16 = bf16[128,5120]{1,0:T(8,128)(2,1)} fusion(bf16[128,5120]{1,0:T(8,128)(2,1)} %collective-permute-done.16, f32[5120,256]{0,1:T(8,128)} %fusion.33, s32[]{:T(128)S(6)} %select_n.40, bf16[128,5120]{1,0:T(8,128)(2,1)} %get-tuple-element.101), kind=kLoop, calls=%fused_computation.33 | loop fusion | flops 3276800 | bytes 6553604 | tf_op jit(solution)/shard_map/cond/branch_2_fun/add | solution.py:113
  342.9 1.8 fusion.15
  344.7 0.0 slice-start.9
  344.7 0.0 slice-start.10
  344.7 0.0 slice-start.11
  344.7 0.0 collective-permute-done.19.peer_ref
  344.8 12.1 %branch_2_fun.5.rest_0_ = bf16[1536,5120]{1,0:T(8,128)(2,1)} custom-call(bf16[1536,256]{1,0:T(8,128)(2,1)S(1)} %bitcast.122, bf16[256,5120]{1,0:T(8,128)(2,1)S(1)} %constant_dynamic-update-slice_fusion.4.cot_ref, bf16[1536,5120]{1,0:T(8,128)(2,1)} %bitcast.155, bf16[512,5120]{1,0:T(8,128)(2,1)} %collective-permute-done.19.peer_ref, ...), custom_call_target="tpu_custom_call", output_to_operand_aliasing={{}: (4, {})} | custom-call | flops 1342177280 | bytes 15728640 | tf_op jit(solution)/shard_map/cond/branch_2_fun/pallas_call | solution.py:64
  356.9 0.0 collective-permute-done.20.peer_ref
  356.9 0.0 slice-done.8
  356.9 0.0 slice-done.9
  356.9 0.0 slice-done.10
  356.9 0.0 slice-done.11
  357.0 13.3 %branch_2_fun.6.rest_0_ = bf16[1536,5120]{1,0:T(8,128)(2,1)} custom-call(bf16[1536,256]{1,0:T(8,128)(2,1)S(1)} %bitcast.123, bf16[256,5120]{1,0:T(8,128)(2,1)S(1)} %constant_dynamic-update-slice_fusion.4.cot_ref, bf16[1536,5120]{1,0:T(8,128)(2,1)S(1)} %bitcast.158, ...), custom_call_target="tpu_custom_call", output_to_operand_aliasing={{}: (4, {})} | custom-call | flops 2013265920 | bytes 23592960 | tf_op jit(solution)/shard_map/cond/branch_2_fun/pallas_call | solution.py:64
  370.3 0.0 collective-permute-done.21.peer_ref
  370.3 4.4 %branch_2_fun.7 = bf16[1536,5120]{1,0:T(8,128)(2,1)} custom-call(bf16[1536,256]{1,0:T(8,128)(2,1)S(1)} %bitcast.124, bf16[256,5120]{1,0:T(8,128)(2,1)S(1)} %constant_dynamic-update-slice_fusion.4.cot_ref, bf16[1536,5120]{1,0:T(8,128)(2,1)S(1)} %bitcast.159, bf16[128,5120]{1,0:T(8,128)(2,1)} %collective-permute-done.21.peer_ref, ...), custom_call_target="tpu_custom_call", output_to_operand_aliasing={{}: (4, {})} | custom-call | flops 335544320 | bytes 3932160 | tf_op jit(solution)/shard_map/cond/branch_2_fun/pallas_call | solution.py:64
  374.6 0.0 collective-permute-done.23
  374.6 2.1 fusion.19
  (2 shorter events, 0.0 us)
Async XLA Ops:
  3.3 303.6 %collective-permute-start.17 = (bf16[128,5120]{1,0:T(8,128)(2,1)}, bf16[128,5120]{1,0:T(8,128)(2,1)}, u32[]{:S(2)}, u32[]{:S(2)}) collective-permute-start(bf16[128,5120]{1,0:T(8,128)(2,1)} %get-tuple-element.105), channel_id=1, source_target_pairs={{1,0},{0,1},{3,2},{2,3},{5,4},{4,5},{7,6},{6,7},{9,8},{8,9},{11,10... | collective-permute-start | bytes 3932168 | tf_op jit(solution)/shard_map/cond/branch_2_fun/ppermute | solution.py:28
  6.3 303.4 %collective-permute-start.18 = (bf16[64,5120]{1,0:T(8,128)(2,1)}, bf16[64,5120]{1,0:T(8,128)(2,1)}, u32[]{:S(2)}, u32[]{:S(2)}) collective-permute-start(bf16[64,5120]{1,0:T(8,128)(2,1)} %get-tuple-element.107), channel_id=1, source_target_pairs={{24,0},{26,2},{28,4},{30,6},{0,8},{2,10},{4,12},{6,14},{8,16},{10,... | collective-permute-start | bytes 1966088 | tf_op jit(solution)/shard_map/cond/branch_2_fun/ppermute | solution.py:28
  13.1 331.7 %collective-permute-start.19 = (bf16[512,5120]{1,0:T(8,128)(2,1)}, bf16[512,5120]{1,0:T(8,128)(2,1)}, u32[]{:S(2)}, u32[]{:S(2)}) collective-permute-start(bf16[512,5120]{1,0:T(8,128)(2,1)} %slice.68), channel_id=1, source_target_pairs={{24,0},{26,2},{28,4},{30,6},{0,8},{2,10},{4,12},{6,14},{8,16},{10,... | collective-permute-start | bytes 15728648 | tf_op jit(solution)/shard_map/cond/branch_2_fun/ppermute | solution.py:28
  21.5 335.5 %collective-permute-start.20 = (bf16[768,5120]{1,0:T(8,128)(2,1)}, bf16[768,5120]{1,0:T(8,128)(2,1)}, u32[]{:S(2)}, u32[]{:S(2)}) collective-permute-start(bf16[768,5120]{1,0:T(8,128)(2,1)} %slice.69), channel_id=1, source_target_pairs={{24,0},{26,2},{28,4},{30,6},{0,8},{2,10},{4,12},{6,14},{8,16},{10,... | collective-permute-start | bytes 23592968 | tf_op jit(solution)/shard_map/cond/branch_2_fun/ppermute | solution.py:28
  23.0 282.6 %collective-permute-start.22 = (f32[1]{0:T(128)}, f32[1]{0:T(128)}, u32[]{:S(2)}, u32[]{:S(2)}) collective-permute-start(f32[1]{0:T(128)} %get-tuple-element.103), channel_id=1, source_target_pairs={{24,0},{26,2},{28,4},{30,6},{0,8},{2,10},{4,12},{6,14},{8,16},{10,... | collective-permute-start | bytes 20 | tf_op jit(solution)/shard_map/cond/branch_2_fun/ppermute | solution.py:28
  23.3 9.5 %copy-start.6 = (bf16[256,1536]{1,0:T(8,128)(2,1)S(1)}, bf16[256,1536]{1,0:T(8,128)(2,1)}, u32[]{:S(2)}) copy-start(bf16[256,1536]{1,0:T(8,128)(2,1)} %get-tuple-element.176) | copy-start | bytes 2359300
  32.8 7.1 %copy-start.2 = (bf16[1536,5120]{1,0:T(8,128)(2,1)}, bf16[1536,5120]{1,0:T(8,128)(2,1)S(1)}, u32[]{:S(2)}) copy-start(bf16[1536,5120]{1,0:T(8,128)(2,1)S(1)} %divide_convert_fusion.2) | copy-start | bytes 47185924
  305.6 64.7 %collective-permute-start.21 = (bf16[128,5120]{1,0:T(8,128)(2,1)}, bf16[128,5120]{1,0:T(8,128)(2,1)}, u32[]{:S(2)}, u32[]{:S(2)}) collective-permute-start(bf16[128,5120]{1,0:T(8,128)(2,1)} %slice.70), channel_id=1, source_target_pairs={{24,0},{26,2},{28,4},{30,6},{0,8},{2,10},{4,12},{6,14},{8,16},{10,... | collective-permute-start | bytes 3932168 | tf_op jit(solution)/shard_map/cond/branch_2_fun/ppermute | solution.py:28
  306.9 67.7 %collective-permute-start.23 = (bf16[64,5120]{1,0:T(8,128)(2,1)}, bf16[64,5120]{1,0:T(8,128)(2,1)}, u32[]{:S(2)}, u32[]{:S(2)}) collective-permute-start(bf16[64,5120]{1,0:T(8,128)(2,1)} %slice.73), channel_id=1, source_target_pairs={{24,0},{26,2},{28,4},{30,6},{0,8},{2,10},{4,12},{6,14},{8,16},{10,... | collective-permute-start | bytes 1966088 | tf_op jit(solution)/shard_map/cond/branch_2_fun/ppermute | solution.py:28
  309.7 29.1 %collective-permute-start.16 = (bf16[128,5120]{1,0:T(8,128)(2,1)}, bf16[128,5120]{1,0:T(8,128)(2,1)}, u32[]{:S(2)}, u32[]{:S(2)}) collective-permute-start(bf16[128,5120]{1,0:T(8,128)(2,1)} %fusion.17), channel_id=1, source_target_pairs={{1,0},{0,1},{3,2},{2,3},{5,4},{4,5},{7,6},{6,7},{9,8},{8,9},{11,10... | collective-permute-start | bytes 3932168 | tf_op jit(solution)/shard_map/cond/branch_2_fun/ppermute | solution.py:28
  342.9 14.0 %slice-start.8 = ((s8[15728640]{0:T(1024)(128)(4,1)}), s8[4194304]{0:T(1024)(128)(4,1)S(1)}, s32[]{:S(2)}) async-start(s8[15728640]{0:T(1024)(128)(4,1)} %bitcast.156), calls=%async_computation.8 | async-start | bytes 8388608
  344.7 12.2 %slice-start.9 = ((s8[15728640]{0:T(1024)(128)(4,1)}), s8[4194304]{0:T(1024)(128)(4,1)S(1)}, s32[]{:S(2)}) async-start(s8[15728640]{0:T(1024)(128)(4,1)} %bitcast.156), calls=%async_computation.9 | async-start | bytes 8388608
  344.7 12.2 %slice-start.10 = ((s8[15728640]{0:T(1024)(128)(4,1)}), s8[4194304]{0:T(1024)(128)(4,1)S(1)}, s32[]{:S(2)}) async-start(s8[15728640]{0:T(1024)(128)(4,1)} %bitcast.156), calls=%async_computation.10 | async-start | bytes 8388608
  344.7 12.2 %slice-start.11 = ((s8[15728640]{0:T(1024)(128)(4,1)}), s8[3145728]{0:T(1024)(128)(4,1)S(1)}, s32[]{:S(2)}) async-start(s8[15728640]{0:T(1024)(128)(4,1)} %bitcast.156), calls=%async_computation.11 | async-start | bytes 6291456
